TPU v7x, 32 devices: a whole 2x2x4 slice. The times are simulated.
32 devices in a mesh: fsdp: 8 (over y, x, core), dp: 4 (over z).
Axes of the slice: x: 2, y: 2, z: 4, core: 2. Of those that a mesh axis runs over, the one named last changes fastest.
Arguments:
- tokens: bfloat16 [16384, 4096], P(('fsdp', 'dp')), may hold values from -40 to 40
- cotangent: bfloat16 [16384, 2048], P(('fsdp', 'dp')), may hold values from -20 to 20
- weight: bfloat16 [4096, 2048], P('fsdp'), may hold values from -1 to 1
- left_vector: float32 [4096], P('fsdp'), may hold values from -6 to 6
Outputs:
- layer_out: bfloat16 [16384, 2048], P(('fsdp', 'dp'))
- input_grad: bfloat16 [16384, 4096], P(('fsdp', 'dp'))
- update: bfloat16 [4096, 2048], P('fsdp')
- left_next: float32 [4096], P('fsdp')
- right_next: float32 [2048], replicated
All inputs are finite; a program needn't handle non-finite values.
Results may differ from a plain program's by a relative error of at most 0.015.
Values may be sent and summed in bfloat16 or wider, within the bound.
A program may use at most 128 MiB of HBM per device.

v0:
```python
import jax
import jax.numpy as jnp
from jax import lax
from jax.sharding import PartitionSpec as P

epsilon = 1e-06


def per_device(tokens, cotangent, weight, left_vector):
    highest = lax.Precision.HIGHEST
    weight_wide = weight.astype(jnp.float32)
    part_right = jnp.dot(left_vector, weight_wide, precision=highest)
    right_raw = lax.psum(part_right, "fsdp")
    right_next = right_raw / jnp.sqrt(jnp.sum(right_raw * right_raw) + epsilon)
    left_raw = jnp.dot(weight_wide, right_next, precision=highest)
    left_sq = lax.psum(jnp.sum(left_raw * left_raw), "fsdp")
    spectral = jnp.sqrt(left_sq + epsilon)
    left_next = left_raw / spectral
    gathered = lax.all_gather(weight, "fsdp", axis=0, tiled=True)
    product = jnp.dot(tokens, gathered, preferred_element_type=jnp.float32)
    layer_out = (product / spectral).astype(jnp.bfloat16)
    back_prod = lax.dot_general(
        cotangent, gathered, (((1,), (1,)), ((), ())), preferred_element_type=jnp.float32
    )
    input_grad = (back_prod / spectral).astype(jnp.bfloat16)
    shard_rows = weight.shape[0]
    shard_sum = lax.psum_scatter(
        lax.dot_general(
            tokens, cotangent, (((0,), (0,)), ((), ())), preferred_element_type=jnp.float32
        ).astype(jnp.bfloat16),
        "fsdp",
        scatter_dimension=0,
        tiled=True,
    )
    grad_sum = lax.psum(shard_sum, "dp").astype(jnp.float32)
    entry_count = shard_rows * lax.axis_size("fsdp") * weight.shape[1]
    along_right = jnp.dot(grad_sum, right_next, precision=highest)
    grad_sq_raw, inner_prod, cross_term = lax.psum(
        (
            jnp.sum(grad_sum * grad_sum),
            jnp.sum(grad_sum * weight_wide),
            jnp.sum(left_next * along_right),
        ),
        "fsdp",
    )
    rank_coeff = inner_prod / (spectral * spectral)
    gradient = grad_sum / spectral - rank_coeff * left_next[:, None] * right_next[None, :]
    left_unit = left_sq / (left_sq + epsilon)
    right_unit = jnp.sum(right_next * right_next)
    grad_sq = (
        grad_sq_raw / (spectral * spectral)
        - 2.0 * rank_coeff * cross_term / spectral
        + rank_coeff * rank_coeff * left_unit * right_unit
    )
    grad_rms = jnp.sqrt(grad_sq / entry_count + epsilon)
    update = (gradient / grad_rms).astype(jnp.bfloat16)
    return (layer_out, input_grad, update, left_next, right_next)


def solution(mesh):
    placed = (P(("fsdp", "dp"), None), P(("fsdp", "dp"), None), P("fsdp", None), P("fsdp"))
    return jax.shard_map(
        per_device,
        mesh=mesh,
        in_specs=placed,
        out_specs=(
            P(("fsdp", "dp"), None),
            P(("fsdp", "dp"), None),
            P("fsdp", None),
            P("fsdp"),
            P(),
        ),
        check_vma=False,
    )
```

profile of v0, /device:TPU:0, one launch (start us, length us, event | category | flops | bytes accessed | tf_op | source)
XLA Modules:
  0.0 355.8 jit_solution(14946485540148376440)
XLA Ops:
  7.2 0.0 reduce-scatter.2.cloned.1.call-start
  7.2 1.5 copy-done
  8.8 14.6 %convolution_convert_fusion = bf16[4096,2048]{1,0:T(8,128)(2,1)} fusion(bf16[512,4096]{1,0:T(8,128)(2,1)} %param.4, bf16[512,2048]{1,0:T(8,128)(2,1)S(1)} %copy-done), kind=kOutput, calls=%fused_computation | convolution fusion | flops 8598323200 | bytes 23068672 | tf_op jit(solution)/shard_map/dot_general | solution.py:28
  23.4 0.0 reduce-scatter.2.cloned.1.call-update
  23.4 0.0 all-reduce.3.cloned.1.call-start
  23.5 119.0 %reduce-scatter.2.cloned.1.call-done = bf16[512,2048]{1,0:T(8,128)(2,1)} async-done(((bf16[4096,2048]{1,0:T(8,128)(2,1)}), bf16[512,2048]{1,0:T(8,128)(2,1)}) %reduce-scatter.2.cloned.1.call-update) | async-done | bytes 2097168 | tf_op jit(solution)/shard_map/reduce_scatter | solution.py:27
  142.5 0.0 all-gather.2.cloned.1.call-start
  142.5 0.7 all-gather.2.cloned.1.call-update
  143.2 2.5 fusion.5
  145.7 13.2 %psum.42 = f32[2048]{0:T(1024)S(1)} all-reduce(f32[2048]{0:T(1024)S(1)} %bitcast.20), channel_id=1, replica_groups=mesh['fsdp'=8,'dp'=4] {'fsdp'}, use_global_device_ids=true, to_apply=%region_0.0 | all-reduce | flops 2048 | bytes 16384 | tf_op jit(solution)/shard_map/psum | solution.py:13
  158.9 0.6 multiply_reduce_fusion.1
  160.2 0.6 multiply_reduce_fusion
  160.8 3.3 fusion.6
  164.1 0.6 multiply_reduce_fusion.3
  164.7 13.2 %psum.43 = f32[]{:T(128)} all-reduce(f32[]{:T(128)} %multiply_reduce_fusion.3), channel_id=1, replica_groups=mesh['fsdp'=8,'dp'=4] {'fsdp'}, use_global_device_ids=true, to_apply=%region_3.0 | all-reduce | flops 1 | bytes 8 | tf_op jit(solution)/shard_map/psum | solution.py:16
  179.3 51.7 %all-reduce.3.cloned.1.call-done = bf16[512,2048]{1,0:T(8,128)(2,1)} async-done(((bf16[512,2048]{1,0:T(8,128)(2,1)}), bf16[512,2048]{1,0:T(8,128)(2,1)}) %all-reduce.3.cloned.1.call-update) | async-done | bytes 2097168 | tf_op jit(solution)/shard_map/psum | solution.py:35
  231.0 3.3 fusion.7
  234.3 0.6 multiply_reduce_fusion.2
  235.0 4.0 %fusion.2 = (f32[]{:T(128)}, f32[]{:T(128)}) fusion(bf16[512,2048]{1,0:T(8,128)(2,1)} %all-reduce.3.cloned.1.call-done, bf16[512,2048]{1,0:T(8,128)(2,1)} %param.6), kind=kLoop, calls=%fused_computation.7 | loop fusion | flops 6291454 | bytes 4194312 | tf_op jit(solution)/shard_map/reduce_sum | solution.py:41
  239.0 15.1 %all-reduce = (f32[]{:T(128)}, f32[]{:T(128)}, f32[]{:T(128)}) all-reduce(f32[]{:T(128)} %get-tuple-element.6, f32[]{:T(128)} %get-tuple-element.5, f32[]{:T(128)} %get-tuple-element.12), channel_id=1, replica_groups=mesh['fsdp'=8,'dp'=4] {'fsdp'}, use_global_device_ids=true, to_apply=%region_9.0 | all-reduce | flops 3 | bytes 24 | tf_op jit(solution)/shard_map/psum | solution.py:38
  256.8 3.7 %fusion.4 = bf16[512,2048]{1,0:T(8,128)(2,1)} fusion(bf16[512,2048]{1,0:T(8,128)(2,1)} %all-reduce.3.cloned.1.call-done, f32[]{:T(128)S(6)} %sqrt.11, f32[2048]{0:T(1024)S(1)} %get-tuple-element.11, f32[512]{0:T(512)S(1)} %broadcast_multiply_fusion, f32[]{:T(128)S(6)} %sqrt.10), kind=kLoop, calls=%fused_computation.9 | loop fusion | flops 6291456 | bytes 4204552 | tf_op jit(solution)/shard_map/convert_element_type | solution.py:56
  260.5 61.3 %all-gather.2.cloned.1.call-done = bf16[4096,2048]{1,0:T(8,128)(2,1)} async-done(((bf16[512,2048]{1,0:T(8,128)(2,1)}), bf16[4096,2048]{1,0:T(8,128)(2,1)}) %all-gather.2.cloned.1.call-update) | async-done | bytes 16777232 | tf_op jit(solution)/shard_map/all_gather | solution.py:19
  321.8 13.9 %divide_convert_fusion = bf16[512,4096]{1,0:T(8,128)(2,1)} fusion(bf16[512,2048]{1,0:T(8,128)(2,1)S(1)} %copy-done, bf16[4096,2048]{1,0:T(8,128)(2,1)} %all-gather.2.cloned.1.call-done, f32[]{:T(128)S(6)} %sqrt.10), kind=kOutput, calls=%fused_computation.1 | convolution fusion | flops 8594128896 | bytes 23068676 | tf_op jit(solution)/shard_map/dot_general | solution.py:22
  335.7 13.5 %divide_convert_fusion.1 = bf16[512,2048]{1,0:T(8,128)(2,1)} fusion(bf16[512,4096]{1,0:T(8,128)(2,1)S(1)} %copy-done.4, bf16[4096,2048]{1,0:T(8,128)(2,1)} %all-gather.2.cloned.1.call-done, f32[]{:T(128)S(6)} %sqrt.10), kind=kOutput, calls=%fused_computation.10 | convolution fusion | flops 8592031744 | bytes 23068676 | tf_op jit(solution)/shard_map/dot_general | solution.py:20
  (11 shorter events, 0.0 us)
Async XLA Ops:
  7.2 1.6 copy-start
  7.2 135.3 %reduce-scatter.2.cloned.1.call-start = ((), (), s32[]{:S(2)}) async-start(), calls=%async_computation.2 | async-start | bytes 18874368 | tf_op jit(solution)/shard_map/reduce_scatter | solution.py:27
  23.4 119.8 %copy-start.3 = (f32[512]{0:T(512)S(1)}, f32[512]{0:T(512)}, u32[]{:S(2)}) copy-start(f32[512]{0:T(512)} %param.7) | copy-start | bytes 6148
  23.4 207.6 %all-reduce.3.cloned.1.call-start = ((), (), s32[]{:S(2)}) async-start(), calls=%async_computation.3 | async-start | bytes 4194304 | tf_op jit(solution)/shard_map/psum | solution.py:35
  142.5 179.3 %all-gather.2.cloned.1.call-start = ((), (), s32[]{:S(2)}) async-start(), calls=%async_computation.1 | async-start | bytes 18874368 | tf_op jit(solution)/shard_map/all_gather | solution.py:19
  160.8 96.0 %copy-start.1 = (f32[2048]{0:T(1024)}, f32[2048]{0:T(1024)S(1)}, u32[]{:S(2)}) copy-start(f32[2048]{0:T(1024)S(1)} %get-tuple-element.11) | copy-start | bytes 24580
  235.0 25.5 %copy-start.2 = (f32[512]{0:T(512)}, f32[512]{0:T(512)S(1)}, u32[]{:S(2)}) copy-start(f32[512]{0:T(512)S(1)} %get-tuple-element.13) | copy-start | bytes 6148
  321.8 13.9 %copy-start.4 = (bf16[512,4096]{1,0:T(8,128)(2,1)S(1)}, bf16[512,4096]{1,0:T(8,128)(2,1)}, u32[]{:S(2)}) copy-start(bf16[512,4096]{1,0:T(8,128)(2,1)} %param.4) | copy-start | bytes 12582916
Sparse Core Ops, SparseCore 0:
  23.5 118.8 reduce-scatter.1
  144.8 86.1 all-reduce.2
  232.9 88.8 all-gather.1
where the time goes:
time: 356 us
  waiting for transfers between devices  233 us (65%)
  matrix products  51.2 us (14%)
  blocking collectives  41.4 us (12%)
  between operations  18.5 us (5%)
  other arithmetic  10.2 us (3%)
    reduce_scatter x1, waiting for transfers between devices, per_device(): lax.psum_scatter(lax.dot_general(tokens, cotangent, (((0,), (0,)), ((), (...  119 us
    all_gather x1, waiting for transfers between devices, per_device(): gathered = lax.all_gather(weight, 'fsdp', axis=0, tiled=True)  61.3 us
    psum x1, waiting for transfers between devices, per_device(): grad_sum = lax.psum(shard_sum, 'dp').astype(jnp.float32)  51.7 us
    psum x1, blocking collectives, per_device(): lax.psum((jnp.sum(grad_sum * grad_sum), jnp.sum(grad_sum * weight_wide),...  15.1 us
    dot_general x1, matrix products, per_device(): lax.dot_general(tokens, cotangent, (((0,), (0,)), ((), ())), preferred_el...  14.6 us
    dot_general x1, matrix products, per_device(): lax.dot_general(cotangent, gathered, (((1,), (1,)), ((), ())), preferred_...  13.9 us
    dot_general x1, matrix products, per_device(): product = jnp.dot(tokens, gathered, preferred_element_type=jnp.float32)  13.5 us
    psum x1, blocking collectives, per_device(): left_sq = lax.psum(jnp.sum(left_raw * left_raw), 'fsdp')  13.2 us
  transfers between devices with their start and end apart: 3, of which 3 were waited for; matrix products, arithmetic and copies ran while one was open for 5% of the time, Pallas kernels for 0%

commit v1 on v0

--- a/solution.py
+++ b/solution.py
@@ -32,7 +32,7 @@
         scatter_dimension=0,
         tiled=True,
     )
-    grad_sum = lax.psum(shard_sum, "dp").astype(jnp.float32)
+    grad_sum = jnp.sum(lax.all_gather(shard_sum, "dp"), axis=0).astype(jnp.float32)
     entry_count = shard_rows * lax.axis_size("fsdp") * weight.shape[1]
     along_right = jnp.dot(grad_sum, right_next, precision=highest)
     grad_sq_raw, inner_prod, cross_term = lax.psum(

time: 356 us -> 429 us (1.21)
  waiting for transfers between devices: 233 us -> 298 us
  other arithmetic: 10.2 us -> 17.5 us
    all_gather x0 -> x1, waiting for transfers between devices: none -> 124 us  [per_device(): lax.all_gather(shard_sum, 'dp')]
    psum x1 -> x0, waiting for transfers between devices: 51.7 us -> none  [per_device(): grad_sum = lax.psum(shard_sum, 'dp').astype(jnp.float32)]
    reduce_sum x0 -> x1, other arithmetic: none -> 7.2 us  [per_device(): jnp.sum(lax.all_gather(shard_sum, 'dp'), axis=0).astype(jnp.float32)]
    all_gather x1, waiting for transfers between devices: 61.3 us -> 55.7 us  [per_device(): gathered = lax.all_gather(weight, 'fsdp', axis=0, tiled=True)]
  transfers between devices with their start and end apart: 3 -> 3, of which waited for: 3 -> 3; matrix products, arithmetic and copies ran while one was open for 5% -> 8% of each run, Pallas kernels for 0% -> 0%
where the time goes in v1:
time: 429 us; the launch traced here: 428 us
  waiting for transfers between devices  298 us (69%)
  matrix products  51.4 us (12%)
  blocking collectives  40.7 us (9%)
  between operations  18.4 us (4%)
  other arithmetic  17.5 us (4%)
    all_gather x1, waiting for transfers between devices, per_device(): lax.all_gather(shard_sum, 'dp')  124 us
    reduce_scatter x1, waiting for transfers between devices, per_device(): lax.psum_scatter(lax.dot_general(tokens, cotangent, (((0,), (0,)), ((), (...  118 us
    all_gather x1, waiting for transfers between devices, per_device(): gathered = lax.all_gather(weight, 'fsdp', axis=0, tiled=True)  55.7 us
    dot_general x1, matrix products, per_device(): lax.dot_general(tokens, cotangent, (((0,), (0,)), ((), ())), preferred_el...  14.6 us
    psum x1, blocking collectives, per_device(): lax.psum((jnp.sum(grad_sum * grad_sum), jnp.sum(grad_sum * weight_wide),...  14.5 us
    dot_general x1, matrix products, per_device(): lax.dot_general(cotangent, gathered, (((1,), (1,)), ((), ())), preferred_...  13.9 us
    dot_general x1, matrix products, per_device(): product = jnp.dot(tokens, gathered, preferred_element_type=jnp.float32)  13.7 us
    psum x1, blocking collectives, per_device(): left_sq = lax.psum(jnp.sum(left_raw * left_raw), 'fsdp')  13.4 us
  transfers between devices with their start and end apart: 3, of which 3 were waited for; matrix products, arithmetic and copies ran while one was open for 8% of the time, Pallas kernels for 0%

profile of v1, /device:TPU:0, one launch (start us, length us, event | category | flops | bytes accessed | tf_op | source)
XLA Modules:
  0.0 428.0 jit_solution(16719236791269977827)
XLA Ops:
  7.2 0.0 reduce-scatter.2.cloned.1.call-start
  7.2 1.5 copy-done
  8.8 14.6 %convolution_convert_fusion = bf16[4096,2048]{1,0:T(8,128)(2,1)} fusion(bf16[512,4096]{1,0:T(8,128)(2,1)} %param.4, bf16[512,2048]{1,0:T(8,128)(2,1)S(1)} %copy-done), kind=kOutput, calls=%fused_computation | convolution fusion | flops 8598323200 | bytes 23068672 | tf_op jit(solution)/shard_map/dot_general | solution.py:28
  23.4 0.0 all-gather.4.cloned.1.call-start
  23.5 0.7 all-gather.4.cloned.1.call-update
  24.2 0.0 all-gather.6.cloned.1.call-start
  24.2 118.2 %reduce-scatter.2.cloned.1.call-done = bf16[512,2048]{1,0:T(8,128)(2,1)} async-done(((bf16[4096,2048]{1,0:T(8,128)(2,1)}), bf16[512,2048]{1,0:T(8,128)(2,1)}) %reduce-scatter.2.cloned.1.call-update) | async-done | bytes 2097168 | tf_op jit(solution)/shard_map/reduce_scatter | solution.py:27
  142.5 2.5 fusion.5
  145.0 12.9 %psum.35 = f32[2048]{0:T(1024)S(1)} all-reduce(f32[2048]{0:T(1024)S(1)} %bitcast.22), channel_id=1, replica_groups=mesh['fsdp'=8,'dp'=4] {'fsdp'}, use_global_device_ids=true, to_apply=%region_0.0 | all-reduce | flops 2048 | bytes 16384 | tf_op jit(solution)/shard_map/psum | solution.py:13
  157.9 0.6 multiply_reduce_fusion.1
  159.2 0.6 multiply_reduce_fusion
  159.8 3.3 fusion.6
  163.1 0.6 multiply_reduce_fusion.3
  163.7 13.4 %psum.36 = f32[]{:T(128)} all-reduce(f32[]{:T(128)} %multiply_reduce_fusion.3), channel_id=1, replica_groups=mesh['fsdp'=8,'dp'=4] {'fsdp'}, use_global_device_ids=true, to_apply=%region_3.0 | all-reduce | flops 1 | bytes 8 | tf_op jit(solution)/shard_map/psum | solution.py:16
  178.5 55.7 %all-gather.4.cloned.1.call-done = bf16[4096,2048]{1,0:T(8,128)(2,1)} async-done(((bf16[512,2048]{1,0:T(8,128)(2,1)}), bf16[4096,2048]{1,0:T(8,128)(2,1)}) %all-gather.4.cloned.1.call-update) | async-done | bytes 16777232 | tf_op jit(solution)/shard_map/all_gather | solution.py:19
  234.2 13.9 %divide_convert_fusion = bf16[512,4096]{1,0:T(8,128)(2,1)} fusion(bf16[512,2048]{1,0:T(8,128)(2,1)S(1)} %copy-done, bf16[4096,2048]{1,0:T(8,128)(2,1)} %all-gather.4.cloned.1.call-done, f32[]{:T(128)S(6)} %sqrt.10), kind=kOutput, calls=%fused_computation.1 | convolution fusion | flops 8594128896 | bytes 23068676 | tf_op jit(solution)/shard_map/dot_general | solution.py:22
  248.2 13.7 %divide_convert_fusion.1 = bf16[512,2048]{1,0:T(8,128)(2,1)} fusion(bf16[512,4096]{1,0:T(8,128)(2,1)S(1)} %copy-done.4, bf16[4096,2048]{1,0:T(8,128)(2,1)} %all-gather.4.cloned.1.call-done, f32[]{:T(128)S(6)} %sqrt.10), kind=kOutput, calls=%fused_computation.10 | convolution fusion | flops 8592031744 | bytes 23068676 | tf_op jit(solution)/shard_map/dot_general | solution.py:20
  261.9 123.6 %all-gather.6.cloned.1.call-done = bf16[2048,2048]{1,0:T(8,128)(2,1)} async-done(((bf16[512,2048]{1,0:T(8,128)(2,1)}), bf16[2048,2048]{1,0:T(8,128)(2,1)}) %all-gather.6.cloned.1.call-update) | async-done | bytes 8388624 | tf_op jit(solution)/shard_map/all_gather | solution.py:35
  385.5 7.2 %reduce_sum.68 = bf16[512,2048]{1,0:T(8,128)(2,1)} reduce(bf16[4,512,2048]{2,1,0:T(8,128)(2,1)} %bitcast.19, bf16[]{:T(256)} %constant.8.clone.1), dimensions={0}, to_apply=%region_5.0 | reduce | flops 3145728 | bytes 10485762 | tf_op jit(solution)/shard_map/reduce_sum | solution.py:35
  392.7 3.3 fusion.7
  396.0 4.1 fusion.2
  400.1 0.6 multiply_reduce_fusion.2
  400.7 14.5 %all-reduce = (f32[]{:T(128)}, f32[]{:T(128)}, f32[]{:T(128)}) all-reduce(f32[]{:T(128)} %get-tuple-element.6, f32[]{:T(128)} %get-tuple-element.5, f32[]{:T(128)} %get-tuple-element.12), channel_id=1, replica_groups=mesh['fsdp'=8,'dp'=4] {'fsdp'}, use_global_device_ids=true, to_apply=%region_9.0 | all-reduce | flops 3 | bytes 24 | tf_op jit(solution)/shard_map/psum | solution.py:38
  417.8 3.7 fusion.4
  (12 shorter events, 0.1 us)
Async XLA Ops:
  7.2 1.6 copy-start
  7.2 135.3 %reduce-scatter.2.cloned.1.call-start = ((), (), s32[]{:S(2)}) async-start(), calls=%async_computation.2 | async-start | bytes 18874368 | tf_op jit(solution)/shard_map/reduce_scatter | solution.py:27
  23.4 119.1 %copy-start.3 = (f32[512]{0:T(512)S(1)}, f32[512]{0:T(512)}, u32[]{:S(2)}) copy-start(f32[512]{0:T(512)} %param.7) | copy-start | bytes 6148
  23.4 210.8 %all-gather.4.cloned.1.call-start = ((), (), s32[]{:S(2)}) async-start(), calls=%async_computation.1 | async-start | bytes 18874368 | tf_op jit(solution)/shard_map/all_gather | solution.py:19
  24.2 361.3 %all-gather.6.cloned.1.call-start = ((), (), s32[]{:S(2)}) async-start(), calls=%async_computation.3 | async-start | bytes 10485760 | tf_op jit(solution)/shard_map/all_gather | solution.py:35
  159.8 258.0 %copy-start.1 = (f32[2048]{0:T(1024)}, f32[2048]{0:T(1024)S(1)}, u32[]{:S(2)}) copy-start(f32[2048]{0:T(1024)S(1)} %get-tuple-element.11) | copy-start | bytes 24580
  234.2 13.9 %copy-start.4 = (bf16[512,4096]{1,0:T(8,128)(2,1)S(1)}, bf16[512,4096]{1,0:T(8,128)(2,1)}, u32[]{:S(2)}) copy-start(bf16[512,4096]{1,0:T(8,128)(2,1)} %param.4) | copy-start | bytes 12582916
  400.7 20.8 %copy-start.2 = (f32[512]{0:T(512)}, f32[512]{0:T(512)S(1)}, u32[]{:S(2)}) copy-start(f32[512]{0:T(512)S(1)} %get-tuple-element.13) | copy-start | bytes 6148
Sparse Core Ops, SparseCore 0:
  23.5 118.8 reduce-scatter.1
  144.3 89.8 all-gather.3
  235.8 149.5 all-gather.5
